TPU v7x, 32 devices: a whole 2x2x4 slice. The times are simulated.
32 devices in a mesh: seq: 16 (over z, y, core), dp: 2 (over x).
Axes of the slice: x: 2, y: 2, z: 4, core: 2. Of those that a mesh axis runs over, the one named last changes fastest.
Arguments:
- q_student: bfloat16 [2, 8192, 1536], P('dp', 'seq'), may hold values from -8 to 8
- kv_student: bfloat16 [2, 128, 3072], P('dp', 'seq'), may hold values from -8 to 8
- q_target: bfloat16 [2, 8192, 1536], P('dp', 'seq'), may hold values from -8 to 8
- kv_target: bfloat16 [2, 128, 3072], P('dp', 'seq'), may hold values from -8 to 8
Outputs:
- student_out: bfloat16 [2, 8192, 1536], P('dp', 'seq')
- target_out: bfloat16 [2, 8192, 1536], P('dp', 'seq')
- distill_loss: float32 [], replicated
All inputs are finite; a program needn't handle non-finite values.
Results may differ from a plain program's by a relative error of at most 0.004.
Values may be sent and summed in bfloat16 or wider, within the bound.
A program may use at most 128 MiB of HBM per device.

v0:
```python
import jax
import jax.numpy as jnp
from jax import lax
from jax.sharding import PartitionSpec as P

HEADS = 12
HD = 128


def absorb(query3, carried, incoming):
    running_max, running_sum, running_out = carried
    block_pairs = incoming[0]
    key_rows = block_pairs.shape[0]
    feature_width = HEADS * HD
    key_block = block_pairs[:, :feature_width].reshape(key_rows, HEADS, HD)
    value_block = block_pairs[:, feature_width:].reshape(key_rows, HEADS, HD)
    scores = jnp.einsum("qhd,khd->hqk", query3, key_block, preferred_element_type=jnp.float32) * (
        1.0 / HD**0.5
    )
    new_max = jnp.maximum(running_max, jnp.max(scores, axis=-1))
    shrink = jnp.exp(running_max - new_max)
    exponent = jnp.exp(scores - new_max[:, :, None])
    running_sum = jnp.sum(exponent, axis=-1)
    running_out = jnp.einsum(
        "hqk,khd->hqd",
        exponent.astype(jnp.bfloat16),
        value_block,
        preferred_element_type=jnp.float32,
    )
    return (new_max, running_sum, running_out)


def normalize(carried, query_rows):
    running_max, running_sum, running_out = carried
    mixed_rows = running_out / running_sum[:, :, None]
    return jnp.transpose(mixed_rows, (1, 0, 2)).reshape(query_rows, HEADS * HD)


def body(q_student, kv_student, q_target, kv_target):
    query_rows = q_student.shape[1]
    student_query = q_student[0].reshape(query_rows, HEADS, HD)
    target_query = q_target[0].reshape(query_rows, HEADS, HD)
    initial = (
        jnp.full((HEADS, query_rows), -1e30, jnp.float32),
        jnp.zeros((HEADS, query_rows), jnp.float32),
        jnp.zeros((HEADS, query_rows, HD), jnp.float32),
    )
    student_all = lax.all_gather(kv_student, "seq", axis=1, tiled=True)
    target_all = lax.all_gather(kv_target, "seq", axis=1, tiled=True)
    student_carry = absorb(student_query, initial, student_all)
    target_carry = absorb(target_query, initial, target_all)
    student_rows = normalize(student_carry, query_rows)
    target_rows = normalize(target_carry, query_rows)
    seq_count = lax.axis_size("seq")
    all_tokens = query_rows * seq_count
    position = (lax.axis_index("seq") * query_rows + jnp.arange(query_rows)).astype(jnp.float32)
    weight = 1.0 + 2.0 * position / float(max(all_tokens - 1, 1))
    gap_rows = student_rows - target_rows
    local_term = jnp.sum(weight[:, None] * gap_rows * gap_rows) / float(all_tokens * HEADS * HD)
    clip_term = lax.psum(local_term, "seq")
    distill_loss = lax.psum(clip_term, "dp")
    return (
        student_rows[None].astype(jnp.bfloat16),
        target_rows[None].astype(jnp.bfloat16),
        distill_loss,
    )


def solution(mesh):
    return jax.shard_map(
        body,
        mesh=mesh,
        in_specs=(
            P("dp", "seq", None),
            P("dp", "seq", None),
            P("dp", "seq", None),
            P("dp", "seq", None),
        ),
        out_specs=(P("dp", "seq", None), P("dp", "seq", None), P()),
        check_vma=False,
    )
```

profile of v0, /device:TPU:0, one launch (start us, length us, event | category | flops | bytes accessed | tf_op | source)
XLA Modules:
  0.0 106.9 jit_solution(2824079883674600560)
XLA Ops:
  0.6 0.0 copy-start
  0.6 25.9 %all_gather.7 = bf16[1,128,3072]{2,1,0:T(8,128)(2,1)S(1)} all-gather(bf16[1,8,3072]{2,1,0:T(8,128)(2,1)} %param.7), channel_id=1, replica_groups=mesh['seq'=16,'dp'=2] {'seq'}, dimensions={1}, use_global_device_ids=true | all-gather | bytes 835584 | tf_op jit(solution)/shard_map/all_gather | solution.py:49
  26.5 0.4 copy.33
  26.9 0.8 fusion.13
  27.7 0.0 copy-done
  27.7 0.7 copy.32
  28.4 0.0 copy-start.4
  28.4 0.6 multiply_reduce_fusion
  29.1 0.6 fusion.3
  29.6 0.0 copy-done.4
  29.6 0.0 copy-start.6
  29.6 2.5 %bitcast_divide_fusion = f32[512,12,128]{0,2,1:T(8,128)} fusion(bf16[128,12,128]{0,2,1:T(8,128)(2,1)S(1)} %bitcast.31, f32[12,512,128]{1,2,0:T(8,128)S(1)} %get-tuple-element.22, f32[512,12]{0,1:T(8,128)S(1)} %bitcast.33, f32[12,512]{1,0:T(8,128)S(1)} %broadcast_maximum_fusion), kind=kOutput, calls=%fused_computation.2 | convolution fusion | flops 204472320 | bytes 6733824 | tf_op jit(solution)/shard_map/hqk,khd->hqd/dot_general | solution.py:24
  32.2 0.0 copy-done.6
  32.2 0.0 copy-start.1
  32.2 19.7 %all_gather.6 = bf16[1,128,3072]{2,1,0:T(8,128)(2,1)S(1)} all-gather(bf16[1,8,3072]{2,1,0:T(8,128)(2,1)S(1)} %copy-done.6), channel_id=1, replica_groups=mesh['seq'=16,'dp'=2] {'seq'}, dimensions={1}, use_global_device_ids=true | all-gather | bytes 835584 | tf_op jit(solution)/shard_map/all_gather | solution.py:48
  51.9 0.4 copy.28
  52.3 0.8 fusion.14
  53.1 0.0 copy-done.1
  53.1 1.6 %copy.27 = bf16[1,512,1536]{1,2,0:T(8,128)(2,1)} copy(bf16[1,512,1536]{2,1,0:T(8,128)(2,1)S(1)} %copy-done.1) | data formatting | bytes 3145728 | tf_op args[0]
  54.7 2.0 %multiply_reduce_fusion.1 = (f32[12,512]{1,0:T(8,128)S(1)}, f32[12,512,128]{1,2,0:T(8,128)S(1)}) fusion(bf16[512,12,128]{0,2,1:T(8,128)(2,1)} %bitcast.23, bf16[128,12,128]{0,2,1:T(8,128)(2,1)S(1)} %bitcast.29), kind=kOutput, calls=%fused_computation.7 | convolution fusion | flops 202893312 | bytes 5136384 | tf_op jit(solution)/shard_map/qhd,khd->hqk/dot_general | solution.py:17
  56.7 0.0 copy-start.3
  56.7 0.0 copy-start.5
  56.7 0.6 copy-done.5
  57.3 1.2 %fusion.1 = f32[12,512]{1,0:T(8,128)} fusion(f32[12,512,128]{1,2,0:T(8,128)S(1)} %get-tuple-element.20, f32[12,512]{1,0:T(8,128)S(1)} %broadcast_maximum_fusion.1), kind=kLoop, calls=%fused_computation.8 | loop fusion | flops 2353152 | bytes 3194880 | tf_op jit(solution)/shard_map/reduce_sum | solution.py:23
  58.5 0.0 copy-done.3
  58.5 6.3 %fusion = (f32[]{:T(128)}, bf16[512,12,128]{0,2,1:T(8,128)(2,1)}, bf16[512,12,128]{0,2,1:T(8,128)(2,1)}) fusion(f32[512,12,128]{0,2,1:T(8,128)} %bitcast_divide_fusion, f32[512]{0:T(512)S(1)} %multiply_add_fusion, f32[512,12]{0,1:T(8,128)} %bitcast.32, bf16[128,12,128]{0,2,1:T(8,128)(2,1)S(1)} %bitcast.30, f32[12,512,128]{1,2,0:T(8,128)S(1)} %get-tuple-element.20, ...), kind=kOutput, calls=%fused_computation.1 | convolution fusion | flops 209190912 | bytes 9881604 | tf_op jit(solution)/shard_map/hqk,khd->hqd/dot_general | solution.py:24
  64.8 0.0 copy-start.2
  64.8 2.7 %copy.37 = bf16[1,512,1536]{2,1,0:T(8,128)(2,1)} copy(bf16[1,512,1536]{1,2,0:T(8,128)(2,1)} %bitcast.27) | data formatting | bytes 3145728
  67.5 0.0 copy-done.2
  67.5 1.6 %copy.38 = bf16[1,512,1536]{2,1,0:T(8,128)(2,1)} copy(bf16[1,512,1536]{1,2,0:T(8,128)(2,1)S(1)} %bitcast.26) | data formatting | bytes 3145728
  69.7 31.7 %psum.14 = f32[]{:T(128)} all-reduce(f32[]{:T(128)S(6)} %div.39), channel_id=1, replica_groups=mesh['seq'=16,'dp'=2] {'seq'}, use_global_device_ids=true, to_apply=%region_5.0 | all-reduce | flops 1 | bytes 8 | tf_op jit(solution)/shard_map/psum | solution.py:60
  101.4 5.5 %psum.15 = f32[]{:T(128)} all-reduce(f32[]{:T(128)} %psum.14), channel_id=1, replica_groups=mesh['seq'=16,'dp'=2] {'dp'}, use_global_device_ids=true, to_apply=%region_6.0 | all-reduce | flops 1 | bytes 8 | tf_op jit(solution)/shard_map/psum | solution.py:61
  (3 shorter events, 0.0 us)
Async XLA Ops:
  0.6 27.1 %copy-start = (bf16[1,512,1536]{2,1,0:T(8,128)(2,1)S(1)}, bf16[1,512,1536]{2,1,0:T(8,128)(2,1)}, u32[]{:S(2)}) copy-start(bf16[1,512,1536]{2,1,0:T(8,128)(2,1)} %param.6) | copy-start | bytes 4718596
  28.4 1.2 %copy-start.4 = (bf16[128,1536]{0,1:T(8,128)(2,1)S(1)}, bf16[128,1536]{0,1:T(8,128)(2,1)}, u32[]{:S(2)}) copy-start(bf16[128,1536]{0,1:T(8,128)(2,1)} %get-tuple-element.16) | copy-start | bytes 1179652
  29.6 2.5 %copy-start.6 = (bf16[1,8,3072]{2,1,0:T(8,128)(2,1)S(1)}, bf16[1,8,3072]{2,1,0:T(8,128)(2,1)}, u32[]{:S(2)}) copy-start(bf16[1,8,3072]{2,1,0:T(8,128)(2,1)} %param.5) | copy-start | bytes 147460
  32.2 20.9 %copy-start.1 = (bf16[1,512,1536]{2,1,0:T(8,128)(2,1)S(1)}, bf16[1,512,1536]{2,1,0:T(8,128)(2,1)}, u32[]{:S(2)}) copy-start(bf16[1,512,1536]{2,1,0:T(8,128)(2,1)} %param.4) | copy-start | bytes 4718596
  56.7 1.8 %copy-start.3 = (bf16[128,1536]{0,1:T(8,128)(2,1)S(1)}, bf16[128,1536]{0,1:T(8,128)(2,1)}, u32[]{:S(2)}) copy-start(bf16[128,1536]{0,1:T(8,128)(2,1)} %get-tuple-element.18) | copy-start | bytes 1179652
  56.7 0.6 copy-start.5
  64.8 2.7 %copy-start.2 = (bf16[512,12,128]{0,2,1:T(8,128)(2,1)S(1)}, bf16[512,12,128]{0,2,1:T(8,128)(2,1)}, u32[]{:S(2)}) copy-start(bf16[512,12,128]{0,2,1:T(8,128)(2,1)} %get-tuple-element.13) | copy-start | bytes 4718596
where the time goes:
time: 107 us
  blocking collectives  82.8 us (77%)
  matrix products  11.5 us (11%)
  local copies, waits for them, and re-layouts  9.49 us (9%)
  other arithmetic  1.75 us (2%)
  between operations  1.39 us (1%)
    psum x1, blocking collectives, body(): clip_term = lax.psum(local_term, 'seq')  31.7 us
    all_gather x1, blocking collectives, body(): target_all = lax.all_gather(kv_target, 'seq', axis=1, tiled=True)  25.9 us
    all_gather x1, blocking collectives, body(): student_all = lax.all_gather(kv_student, 'seq', axis=1, tiled=True)  19.7 us
    dot_general x2, matrix products, absorb(): jnp.einsum('hqk,khd->hqd', exponent.astype(jnp.bfloat16), value_block, pr...  8.79 us
    unnamed x18, local copies, waits for them, and re-layouts  7.15 us
    psum x1, blocking collectives, body(): distill_loss = lax.psum(clip_term, 'dp')  5.54 us
    dot_general x2, matrix products, absorb(): jnp.einsum('qhd,khd->hqk', query3, key_block, preferred_element_type=jnp....  2.66 us

commit v1 on v0

v1 whole, which is shorter than its diff:
```python
import functools

import jax
import jax.numpy as jnp
from jax import lax
from jax.experimental import pallas as pl
from jax.experimental.pallas import tpu as pltpu
from jax.sharding import PartitionSpec as P

HEADS = 12
HD = 128
FEAT = HEADS * HD
GROUPS = 3
WIDTH = FEAT // GROUPS
PAIR = 2 * HD
ROWS = 128
LOG2E = 1.4426950408889634
MESH = pl.DeviceIdType.MESH


def kernel(
    n, n_dp, q_s, kv_s, q_t, kv_t, out_s, out_t, loss_out,
    q_buf, k_buf, v_buf, loss_acc, loss_all,
    q_sem, own_sem, swap_s, swap_r, ay_s, ay_r, az_s, az_r, ap_s, ap_r,
    bz_s, bz_r, by_s, by_r, bp_s, bp_r, row_sem, loss_s, loss_r,
):
    line = n // 4
    me = lax.axis_index("seq")
    dp = lax.axis_index("dp")
    z, y, c = me // 4, (me // 2) % 2, me % 2
    partner = z * 4 + y * 2 + (1 - c)
    across = z * 4 + (1 - y) * 2 + c
    left, right = me - 4, me + 4

    def at(seq):
        return {"dp": dp, "seq": seq}

    own = []
    for m, ref in enumerate((kv_s, kv_t)):
        own.append(pltpu.make_async_copy(ref.at[0, :, pl.ds(0, FEAT)], k_buf.at[m, me], own_sem.at[m, 0]))
        own.append(pltpu.make_async_copy(ref.at[0, :, pl.ds(FEAT, FEAT)], v_buf.at[m, me], own_sem.at[m, 1]))
    for copy in own:
        copy.start()
    loads = [pltpu.make_async_copy(ref.at[0], q_buf.at[m], q_sem.at[m]) for m, ref in enumerate((q_s, q_t))]
    for copy in loads:
        copy.start()

    barrier = pltpu.get_barrier_semaphore()
    for seq in (partner, across):
        pl.semaphore_signal(barrier, inc=1, device_id=at(seq), device_id_type=MESH)
    for k in range(1, n_dp):
        pl.semaphore_signal(
            barrier, inc=1, device_id={"dp": (dp + k) % n_dp, "seq": me}, device_id_type=MESH
        )

    @pl.when(z > 0)
    def _():
        pl.semaphore_signal(barrier, inc=1, device_id=at(left), device_id_type=MESH)

    @pl.when(z < line - 1)
    def _():
        pl.semaphore_signal(barrier, inc=1, device_id=at(right), device_id_type=MESH)

    sides_here = jnp.where(z > 0, 1, 0) + jnp.where(z < line - 1, 1, 0)
    pl.semaphore_wait(barrier, 1 + n_dp + sides_here)

    for copy in own:
        copy.wait()

    def rdma(ref, send, recv, target):
        return pltpu.make_async_remote_copy(
            src_ref=ref, dst_ref=ref, send_sem=send, recv_sem=recv,
            device_id=at(target), device_id_type=MESH,
        )

    def cols(g):
        return pl.ds(g * WIDTH, WIDTH)

    def quad(g, zz):
        return k_buf.at[c, pl.ds(zz * 4, 4), :, cols(g)]

    def kpair(g, zz, yy, m):
        return k_buf.at[m, pl.ds(zz * 4 + yy * 2, 2), :, cols(g)]

    def vpair(g, zz, yy, m):
        return v_buf.at[m, pl.ds(zz * 4 + yy * 2, 2), :, cols(g)]

    def swap(g, m, part, dev):
        buf = (k_buf, v_buf)[part]
        return rdma(buf.at[m, dev, :, cols(g)], swap_s.at[g, m, part], swap_r.at[g, m, part], partner)

    def a_y(g, yy):
        return rdma(kpair(g, z, yy, c), ay_s.at[g], ay_r.at[g], across)

    def a_z(g, origin, slot, target):
        return rdma(quad(g, origin), az_s.at[g, slot], az_r.at[g, origin], target)

    def a_p(g, origin, m):
        ref = k_buf.at[m, pl.ds(origin * 4, 4), :, cols(g)]
        return rdma(ref, ap_s.at[g, origin], ap_r.at[g, origin], partner)

    def a_py(g, m):
        return rdma(kpair(g, z, 1 - y, m), ap_s.at[g, z], ap_r.at[g, z], partner)

    def b_z(g, origin, slot, target):
        return rdma(vpair(g, origin, y, c), bz_s.at[g, slot], bz_r.at[g, origin], target)

    def b_y(g, origin, yy):
        return rdma(vpair(g, origin, yy, c), by_s.at[g, origin], by_r.at[g, origin], across)

    def b_p(g, origin, yy, flag, m):
        return rdma(vpair(g, origin, yy, m), bp_s.at[g, flag, origin], bp_r.at[g, flag, origin], partner)

    def sides(s, act):
        @pl.when(z - s >= 0)
        def _():
            act(z - s, z + 1 < line, right)

        @pl.when(z + s < line)
        def _():
            act(z + s, z > 0, left)

    def ends(make_copy):
        @pl.when(z + 1 < line)
        def _():
            make_copy(z, right)

        @pl.when(z > 0)
        def _():
            make_copy(line, left)

    def stage(g, t):
        if t == 0:
            for part in range(2):
                for m in range(2):
                    swap(g, m, part, partner).wait_recv()
            a_y(g, y).start()
            ends(lambda slot, target: b_z(g, z, slot, target).start())
            b_y(g, z, y).start()
        if t == 1:
            a_y(g, 1 - y).wait_recv()
            ends(lambda slot, target: a_z(g, z, slot, target).start())
            a_py(g, c).start()
        if 1 <= t < line:
            def act(origin, more, target):
                b_z(g, origin, origin, target).wait_recv()

                @pl.when(more)
                def _():
                    b_z(g, origin, origin, target).start()

                b_y(g, origin, y).start()
                b_p(g, origin, y, 0, c).start()

            sides(t, act)
        if t == 1:
            b_y(g, z, 1 - y).wait_recv()
            b_p(g, z, 1 - y, 1, c).start()
        if 2 <= t <= line:
            def act2(origin, more, target):
                a_z(g, origin, origin, target).wait_recv()

                @pl.when(more)
                def _():
                    a_z(g, origin, origin, target).start()

                a_p(g, origin, c).start()
                b_y(g, origin, 1 - y).wait_recv()
                b_p(g, origin, 1 - y, 1, c).start()

            sides(t - 1, act2)
        if t == line + 1:
            a_py(g, 1 - c).wait_recv()
            b_p(g, z, 1 - y, 1, 1 - c).wait_recv()
            for s in range(1, line):
                def act3(origin, more, target):
                    a_p(g, origin, 1 - c).wait_recv()
                    b_p(g, origin, y, 0, 1 - c).wait_recv()
                    b_p(g, origin, 1 - y, 1, 1 - c).wait_recv()

                sides(s, act3)

    def drain(g):
        for part in range(2):
            for m in range(2):
                swap(g, m, part, me).wait_send()
        a_y(g, y).wait_send()
        a_py(g, c).wait_send()
        b_y(g, z, y).wait_send()
        b_p(g, z, 1 - y, 1, c).wait_send()
        ends(lambda slot, target: a_z(g, z, slot, target).wait_send())
        ends(lambda slot, target: b_z(g, z, slot, target).wait_send())
        for s in range(1, line):
            def act(origin, more, target):
                @pl.when(more)
                def _():
                    a_z(g, origin, origin, target).wait_send()
                    b_z(g, origin, origin, target).wait_send()

                a_p(g, origin, c).wait_send()
                b_y(g, origin, y).wait_send()
                b_p(g, origin, y, 0, c).wait_send()
                b_p(g, origin, 1 - y, 1, c).wait_send()

            sides(s, act)

    keys = n * 8
    rows = q_buf.shape[1]
    total_rows = rows * n
    factor = LOG2E / HD**0.5

    def head_block(buf, m, col):
        block = buf[m, :, :, pl.ds(col, HD)].astype(jnp.float32)
        return block.reshape(keys, HD).astype(jnp.bfloat16)

    def paired(buf, m, col):
        zero = jnp.zeros((keys, HD), jnp.bfloat16)
        top = jnp.concatenate([head_block(buf, m, col), zero], axis=1)
        low = jnp.concatenate([zero, head_block(buf, m, col + HD)], axis=1)
        return jnp.concatenate([top, low], axis=0)

    def compute(g):
        for pair in range(WIDTH // PAIR):
            col = g * WIDTH + pair * PAIR
            mats = [(paired(k_buf, m, col), paired(v_buf, m, col)) for m in range(2)]

            def tile(i, carry):
                base = pl.multiple_of(i * ROWS, ROWS)
                span = pl.ds(base, ROWS)
                mixed = []
                for m in range(2):
                    key2, value2 = mats[m]
                    scores = lax.dot_general(
                        q_buf[m, span, pl.ds(col, PAIR)], key2, (((1,), (1,)), ((), ())),
                        preferred_element_type=jnp.float32,
                    )
                    expo, inverse = [], []
                    for h in range(2):
                        part = scores[:, h * keys : (h + 1) * keys]
                        top = jnp.max(part, axis=-1, keepdims=True)
                        e = jnp.exp2((part - top) * factor)
                        inverse.append(1.0 / jnp.sum(e, axis=-1, keepdims=True))
                        expo.append(e.astype(jnp.bfloat16))
                    out = jnp.dot(
                        jnp.concatenate(expo, axis=1), value2, preferred_element_type=jnp.float32
                    )
                    mixed.append([out[:, h * HD : (h + 1) * HD] * inverse[h] for h in range(2)])
                for m, ref in enumerate((out_s, out_t)):
                    for h in range(2):
                        ref[0, span, pl.ds(col + h * HD, HD)] = mixed[m][h].astype(jnp.bfloat16)
                position = me * rows + base + lax.broadcasted_iota(jnp.int32, (ROWS, HD), 0)
                weight = 1.0 + position.astype(jnp.float32) * (2.0 / max(total_rows - 1, 1))
                gap0 = mixed[0][0] - mixed[1][0]
                gap1 = mixed[0][1] - mixed[1][1]
                term = weight * (gap0 * gap0 + gap1 * gap1)
                loss_acc[...] += jnp.sum(term.reshape(ROWS // 8, 8, HD), axis=0)
                return carry

            lax.fori_loop(0, rows // ROWS, tile, 0, unroll=2)

    loss_acc[...] = jnp.zeros_like(loss_acc)
    for g in range(GROUPS):
        for part in range(2):
            for m in range(2):
                swap(g, m, part, me).start()
    last = line + 1
    for t in range(last + GROUPS):
        for g in range(GROUPS):
            if 0 <= t - g <= last:
                stage(g, t - g)
        if t == last:
            for k in range(1, n_dp):
                pl.semaphore_signal(
                    row_sem, inc=1, device_id={"dp": (dp + k) % n_dp, "seq": me}, device_id_type=MESH
                )
            for copy in loads:
                copy.wait()
        if t >= last:
            compute(t - last)

    flat = dp * n + me
    count = n * n_dp
    loss_all[flat] = jnp.sum(loss_acc[...], axis=0, keepdims=True)
    pl.semaphore_wait(row_sem, n_dp - 1)

    def exchange(source, k, target):
        return pltpu.make_async_remote_copy(
            src_ref=loss_all.at[source], dst_ref=loss_all.at[source],
            send_sem=loss_s.at[k], recv_sem=loss_r.at[k],
            device_id={"dp": target // n, "seq": target % n}, device_id_type=MESH,
        )

    def send(k, carry):
        exchange(flat, k, (flat + k) % count).start()
        return carry

    lax.fori_loop(1, count, send, 0)
    for g in range(GROUPS):
        drain(g)

    def receive(k, carry):
        target = (flat + k) % count
        exchange((flat + count - k) % count, k, target).wait_recv()
        exchange(flat, k, target).wait_send()
        return carry

    lax.fori_loop(1, count, receive, 0)
    total = jnp.sum(loss_all[...]) / float(total_rows * FEAT)
    loss_out[0, 0] = total


def body(n, n_dp, q_student, kv_student, q_target, kv_target):
    rows = q_student.shape[1]
    line = n // 4
    dma = pltpu.SemaphoreType.DMA
    any_spec = pl.BlockSpec(memory_space=pl.ANY)
    vmem_spec = pl.BlockSpec(memory_space=pltpu.VMEM)
    outs = pl.pallas_call(
        functools.partial(kernel, n, n_dp),
        out_shape=(
            jax.ShapeDtypeStruct(q_student.shape, jnp.bfloat16),
            jax.ShapeDtypeStruct(q_student.shape, jnp.bfloat16),
            jax.ShapeDtypeStruct((1, 1), jnp.float32),
        ),
        in_specs=[any_spec] * 4,
        out_specs=(vmem_spec, vmem_spec, pl.BlockSpec(memory_space=pltpu.SMEM)),
        scratch_shapes=[
            pltpu.VMEM((2, rows, FEAT), jnp.bfloat16),
            pltpu.VMEM((2, n, 8, FEAT), jnp.bfloat16),
            pltpu.VMEM((2, n, 8, FEAT), jnp.bfloat16),
            pltpu.VMEM((8, HD), jnp.float32),
            pltpu.VMEM((n * n_dp, 1, HD), jnp.float32),
            dma((2,)),
            dma((2, 2)),
            dma((GROUPS, 2, 2)),
            dma((GROUPS, 2, 2)),
            dma((GROUPS,)),
            dma((GROUPS,)),
            dma((GROUPS, line + 1)),
            dma((GROUPS, line)),
            dma((GROUPS, line)),
            dma((GROUPS, line)),
            dma((GROUPS, line + 1)),
            dma((GROUPS, line)),
            dma((GROUPS, line)),
            dma((GROUPS, line)),
            dma((GROUPS, 2, line)),
            dma((GROUPS, 2, line)),
            pltpu.SemaphoreType.REGULAR,
            dma((n * n_dp,)),
            dma((n * n_dp,)),
        ],
        compiler_params=pltpu.CompilerParams(
            collective_id=0, has_side_effects=True, vmem_limit_bytes=60 * 1024 * 1024
        ),
    )(q_student, kv_student, q_target, kv_target)
    return outs[0], outs[1], outs[2].reshape(())


def solution(mesh):
    n, n_dp = mesh.shape["seq"], mesh.shape["dp"]
    spec = P("dp", "seq", None)
    return jax.shard_map(
        functools.partial(body, n, n_dp),
        mesh=mesh,
        in_specs=(spec,) * 4,
        out_specs=(spec, spec, P()),
        check_vma=False,
    )
```

time: 107 us -> 52.4 us (0.49)
  blocking collectives: 82.8 us -> 0 us
  Pallas kernels: 0 us -> 45.9 us
  matrix products: 11.5 us -> 0 us
  local copies, waits for them, and re-layouts: 9.49 us -> 3.92 us
  other arithmetic: 1.75 us -> 0 us
  between operations: 1.39 us -> 2.47 us
    pallas_call x0 -> x1, Pallas kernels: none -> 45.9 us  [body(): pl.pallas_call(functools.partial(kernel, n, n_dp), out_shape=(jax.ShapeDt...]
    all_gather x2 -> x0, blocking collectives: 45.6 us -> none  [the longest x1 25.9 us: body(): target_all = lax.all_gather(kv_target, 'seq', axis=1, tiled=True)]
    psum x2 -> x0, blocking collectives: 37.3 us -> none  [the longest x1 31.7 us: body(): clip_term = lax.psum(local_term, 'seq')]
    dot_general x4 -> x0, matrix products: 11.5 us -> none  [the longest x2 8.79 us: absorb(): jnp.einsum('hqk,khd->hqd', exponent.astype(jnp.bfloat16), value_block, pr...]
    unnamed x18 -> x4, local copies, waits for them, and re-layouts: 7.15 us -> 3.92 us
    reduce_sum x2 -> x0, other arithmetic: 1.73 us -> none  [absorb(): running_sum = jnp.sum(exponent, axis=-1)]
    slice x2 -> x0, local copies, waits for them, and re-layouts: 1.61 us -> none  [absorb(): key_block = block_pairs[:, :feature_width].reshape(key_rows, HEADS, HD)]
where the time goes in v1:
time: 52.4 us; the launch traced here: 52.2 us
  Pallas kernels  45.9 us (88%)
  local copies, waits for them, and re-layouts  3.92 us (7%)
  between operations  2.47 us (5%)
    pallas_call x1, Pallas kernels, body(): pl.pallas_call(functools.partial(kernel, n, n_dp), out_shape=(jax.ShapeDt...  45.9 us
    unnamed x4, local copies, waits for them, and re-layouts  3.92 us

profile of v1, /device:TPU:0, one launch (start us, length us, event | category | flops | bytes accessed | tf_op | source)
XLA Modules:
  0.0 52.2 jit_solution(15370419949686353770)
XLA Ops:
  0.6 45.9 %shard_map.67 = (bf16[1,512,1536]{2,1,0:T(8,128)(2,1)}, bf16[1,512,1536]{2,1,0:T(8,128)(2,1)}, f32[1,1]{1,0:T(1,128)}) custom-call(bf16[1,512,1536]{2,1,0:T(8,128)(2,1)} %q_s.1, bf16[1,8,3072]{2,1,0:T(8,128)(2,1)} %kv_s.1, bf16[1,512,1536]{2,1,0:T(8,128)(2,1)} %q_t.1, bf16[1,8,3072]{2,1,0:T(8,128)(2,1)} %kv_t.1), custom_call_target="tpu_custom_call" | custom-call | tf_op jit(solution)/shard_map/pallas_call | solution.py:318
  46.5 0.0 copy-start
  46.5 2.8 %copy.10 = bf16[1,512,1536]{2,1,0:T(8,128)(2,1)} copy(bf16[1,512,1536]{2,1,0:T(8,128)(2,1)} %get-tuple-element.12) | data formatting | bytes 3145728
  49.3 0.0 copy-done
  49.3 1.1 %copy.11 = bf16[1,512,1536]{2,1,0:T(8,128)(2,1)} copy(bf16[1,512,1536]{2,1,0:T(8,128)(2,1)S(1)} %copy-done) | data formatting | bytes 3145728
Async XLA Ops:
  46.5 2.8 %copy-start = (bf16[1,512,1536]{2,1,0:T(8,128)(2,1)S(1)}, bf16[1,512,1536]{2,1,0:T(8,128)(2,1)}, u32[]{:S(2)}) copy-start(bf16[1,512,1536]{2,1,0:T(8,128)(2,1)} %get-tuple-element.13) | copy-start | bytes 4718596

commit v2 on v1

--- a/solution.py
+++ b/solution.py
@@ -10,7 +10,7 @@
 HEADS = 12
 HD = 128
 FEAT = HEADS * HD
-GROUPS = 3
+GROUPS = 1
 WIDTH = FEAT // GROUPS
 PAIR = 2 * HD
 ROWS = 128
@@ -318,8 +318,8 @@
     outs = pl.pallas_call(
         functools.partial(kernel, n, n_dp),
         out_shape=(
-            jax.ShapeDtypeStruct(q_student.shape, jnp.bfloat16),
-            jax.ShapeDtypeStruct(q_student.shape, jnp.bfloat16),
+            pltpu.VMEM(q_student.shape, jnp.bfloat16),
+            pltpu.VMEM(q_student.shape, jnp.bfloat16),
             jax.ShapeDtypeStruct((1, 1), jnp.float32),
         ),
         in_specs=[any_spec] * 4,

time: 52.4 us -> 48.3 us (0.922)
  Pallas kernels: 45.9 us -> 43.6 us
  local copies, waits for them, and re-layouts: 3.92 us -> 2.29 us
    pallas_call x1, Pallas kernels: 45.9 us -> 43.6 us  [body(): pl.pallas_call(functools.partial(kernel, n, n_dp), out_shape=(pltpu.VMEM(...]
    unnamed x4 -> x2, local copies, waits for them, and re-layouts: 3.92 us -> 2.29 us
where the time goes in v2:
time: 48.3 us; the launch traced here: 48.2 us
  Pallas kernels  43.6 us (90%)
  between operations  2.33 us (5%)
  local copies, waits for them, and re-layouts  2.29 us (5%)
    pallas_call x1, Pallas kernels, body(): pl.pallas_call(functools.partial(kernel, n, n_dp), out_shape=(pltpu.VMEM(...  43.6 us
    unnamed x2, local copies, waits for them, and re-layouts  2.29 us

profile of v2, /device:TPU:0, one launch (start us, length us, event | category | flops | bytes accessed | tf_op | source)
XLA Modules:
  0.0 48.2 jit_solution(9196312171369925180)
XLA Ops:
  0.6 43.6 %shard_map.67 = (bf16[1,512,1536]{2,1,0:T(8,128)(2,1)S(1)}, bf16[1,512,1536]{2,1,0:T(8,128)(2,1)S(1)}, f32[1,1]{1,0:T(1,128)}) custom-call(bf16[1,512,1536]{2,1,0:T(8,128)(2,1)} %q_s.1, bf16[1,8,3072]{2,1,0:T(8,128)(2,1)} %kv_s.1, bf16[1,512,1536]{2,1,0:T(8,128)(2,1)} %q_t.1, bf16[1,8,3072]{2,1,0:T(8,128)(2,1)} %kv_t.1), custom_call_target="tpu_custom_call" | custom-call | tf_op jit(solution)/shard_map/pallas_call | solution.py:318
  44.2 1.1 %copy.10 = bf16[1,512,1536]{2,1,0:T(8,128)(2,1)} copy(bf16[1,512,1536]{2,1,0:T(8,128)(2,1)S(1)} %get-tuple-element.9) | data formatting | bytes 3145728
  45.3 1.1 %copy.11 = bf16[1,512,1536]{2,1,0:T(8,128)(2,1)} copy(bf16[1,512,1536]{2,1,0:T(8,128)(2,1)S(1)} %get-tuple-element.10) | data formatting | bytes 3145728

commit v3 on v2

v3 whole, which is shorter than its diff:
```python
import functools

import jax
import jax.numpy as jnp
from jax import lax
from jax.experimental import pallas as pl
from jax.experimental.pallas import tpu as pltpu
from jax.sharding import PartitionSpec as P

HEADS = 12
HD = 128
FEAT = HEADS * HD
GROUPS = 3
WIDTH = FEAT // GROUPS
PAIR = 2 * HD
ROWS = 256
LOG2E = 1.4426950408889634
MESH = pl.DeviceIdType.MESH


def kernel(
    n, n_dp, q_s, kv_s, q_t, kv_t, out_s, out_t, loss_out,
    q_buf, buf, loss_acc, loss_all,
    q_sem, own_sem, swap_s, swap_r, z_s, z_r, y_s, y_r, p_s, p_r, row_sem, loss_s, loss_r,
):
    line = n // 4
    me = lax.axis_index("seq")
    dp = lax.axis_index("dp")
    z, y, c = me // 4, (me // 2) % 2, me % 2
    partner = z * 4 + y * 2 + (1 - c)
    across = z * 4 + (1 - y) * 2 + c

    def at(seq):
        return {"dp": dp, "seq": seq}

    def plane(k):
        return (z + k) % line

    own = [
        pltpu.make_async_copy(
            ref.at[0, :, pl.ds(part * FEAT + g * WIDTH, WIDTH)],
            buf.at[m, g, me, part],
            own_sem.at[m, g, part],
        )
        for g in range(GROUPS)
        for m, ref in enumerate((kv_s, kv_t))
        for part in range(2)
    ]
    for copy in own:
        copy.start()
    loads = [pltpu.make_async_copy(ref.at[0], q_buf.at[m], q_sem.at[m]) for m, ref in enumerate((q_s, q_t))]
    for copy in loads:
        copy.start()

    barrier = pltpu.get_barrier_semaphore()
    first = [at(partner), at(across)]
    first += [at(plane(k) * 4 + y * 2 + c) for k in range(1, line)]
    first += [{"dp": (dp + k) % n_dp, "seq": me} for k in range(1, n_dp)]
    for device in first:
        pl.semaphore_signal(barrier, inc=1, device_id=device, device_id_type=MESH)
    pl.semaphore_wait(barrier, len(first))

    for copy in own:
        copy.wait()

    def rdma(ref, send, recv, target):
        return pltpu.make_async_remote_copy(
            src_ref=ref, dst_ref=ref, send_sem=send, recv_sem=recv,
            device_id=at(target), device_id_type=MESH,
        )

    def duo(m, g, zz, yy):
        return buf.at[m, g, pl.ds(zz * 4 + yy * 2, 2)]

    def swap(g, m, dev):
        return rdma(buf.at[m, g, dev], swap_s.at[g, m], swap_r.at[g, m], partner)

    def along(g, k, origin):
        return rdma(duo(c, g, origin, y), z_s.at[g, k], z_r.at[g, k], plane(k) * 4 + y * 2 + c)

    def over(g, k, yy):
        return rdma(duo(c, g, plane(line - k), yy), y_s.at[g, k], y_r.at[g, k], across)

    def share(g, k, side, m):
        yy = y if side == 0 else 1 - y
        ref = duo(m, g, plane(line - k), yy)
        return rdma(ref, p_s.at[g, side, k], p_r.at[g, side, k], partner)

    def relay_z(g):
        for k in range(1, line):
            along(g, k, plane(line - k)).wait_recv()
            over(g, k, y).start()
            share(g, k, 0, c).start()

    def relay_y(g):
        for k in range(line):
            over(g, k, 1 - y).wait_recv()
            share(g, k, 1, c).start()

    def finish(g):
        for k in range(line):
            if k:
                share(g, k, 0, 1 - c).wait_recv()
            share(g, k, 1, 1 - c).wait_recv()

    def drain(g):
        for m in range(2):
            swap(g, m, me).wait_send()
        for k in range(line):
            over(g, k, y).wait_send()
            share(g, k, 1, c).wait_send()
            if k:
                along(g, k, z).wait_send()
                share(g, k, 0, c).wait_send()

    keys = n * 8
    rows = q_buf.shape[1]
    total_rows = rows * n
    factor = LOG2E / HD**0.5

    def head_block(m, g, part, col):
        block = buf[m, g, :, part, :, pl.ds(col, HD)].astype(jnp.float32)
        return block.reshape(keys, HD).astype(jnp.bfloat16)

    def paired(m, g, part, col):
        zero = jnp.zeros((keys, HD), jnp.bfloat16)
        top = jnp.concatenate([head_block(m, g, part, col), zero], axis=1)
        low = jnp.concatenate([zero, head_block(m, g, part, col + HD)], axis=1)
        return jnp.concatenate([top, low], axis=0)

    def compute(g, pair):
            col = g * WIDTH + pair * PAIR
            mats = [
                (paired(m, g, 0, pair * PAIR), paired(m, g, 1, pair * PAIR)) for m in range(2)
            ]

            def tile(i, carry):
                base = i * ROWS
                span = pl.ds(base, ROWS)
                mixed = []
                for m in range(2):
                    key2, value2 = mats[m]
                    scores = lax.dot_general(
                        q_buf[m, span, pl.ds(col, PAIR)], key2, (((1,), (1,)), ((), ())),
                        preferred_element_type=jnp.float32,
                    )
                    expo, inverse = [], []
                    for h in range(2):
                        part = scores[:, h * keys : (h + 1) * keys]
                        top = jnp.max(part, axis=-1, keepdims=True)
                        e = jnp.exp2((part - top) * factor)
                        inverse.append(1.0 / jnp.sum(e, axis=-1, keepdims=True))
                        expo.append(e.astype(jnp.bfloat16))
                    out = jnp.dot(
                        jnp.concatenate(expo, axis=1), value2, preferred_element_type=jnp.float32
                    )
                    mixed.append([out[:, h * HD : (h + 1) * HD] * inverse[h] for h in range(2)])
                for m, ref in enumerate((out_s, out_t)):
                    for h in range(2):
                        ref[0, span, pl.ds(col + h * HD, HD)] = mixed[m][h].astype(jnp.bfloat16)
                position = me * rows + base + lax.broadcasted_iota(jnp.int32, (ROWS, HD), 0)
                weight = 1.0 + position.astype(jnp.float32) * (2.0 / max(total_rows - 1, 1))
                gap0 = mixed[0][0] - mixed[1][0]
                gap1 = mixed[0][1] - mixed[1][1]
                term = weight * (gap0 * gap0 + gap1 * gap1)
                loss_acc[...] += jnp.sum(term.reshape(ROWS // 8, 8, HD), axis=0)
                return carry

            for i in range(rows // ROWS):
                tile(i, 0)

    loss_acc[...] = jnp.zeros_like(loss_acc)
    for g in range(GROUPS):
        for m in range(2):
            swap(g, m, me).start()
    for g in range(GROUPS):
        for m in range(2):
            swap(g, m, partner).wait_recv()
        for k in range(1, line):
            along(g, k, z).start()
        over(g, 0, y).start()
    relay_z(0)
    if GROUPS > 1:
        relay_z(1)
    relay_y(0)
    finish(0)
    for k in range(1, n_dp):
        pl.semaphore_signal(
            row_sem, inc=1, device_id={"dp": (dp + k) % n_dp, "seq": me}, device_id_type=MESH
        )
    for copy in loads:
        copy.wait()
    pairs = WIDTH // PAIR
    for g in range(GROUPS):
        for pair in range(pairs):
            if pair == pairs - 1 and g + 1 < GROUPS:
                relay_y(g + 1)
                if g + 2 < GROUPS:
                    relay_z(g + 2)
            compute(g, pair)
        if g + 1 < GROUPS:
            finish(g + 1)

    flat = dp * n + me
    count = n * n_dp
    loss_all[flat] = jnp.sum(loss_acc[...], axis=0, keepdims=True)
    pl.semaphore_wait(row_sem, n_dp - 1)

    def exchange(source, k, target):
        return pltpu.make_async_remote_copy(
            src_ref=loss_all.at[source], dst_ref=loss_all.at[source],
            send_sem=loss_s.at[k], recv_sem=loss_r.at[k],
            device_id={"dp": target // n, "seq": target % n}, device_id_type=MESH,
        )

    def send(k, carry):
        exchange(flat, k, (flat + k) % count).start()
        return carry

    lax.fori_loop(1, count, send, 0)
    for g in range(GROUPS):
        drain(g)

    def receive(k, carry):
        target = (flat + k) % count
        exchange((flat + count - k) % count, k, target).wait_recv()
        exchange(flat, k, target).wait_send()
        return carry

    lax.fori_loop(1, count, receive, 0)
    total = jnp.sum(loss_all[...]) / float(total_rows * FEAT)
    loss_out[0, 0] = total


def body(n, n_dp, q_student, kv_student, q_target, kv_target):
    rows = q_student.shape[1]
    line = n // 4
    dma = pltpu.SemaphoreType.DMA
    any_spec = pl.BlockSpec(memory_space=pl.ANY)
    vmem_spec = pl.BlockSpec(memory_space=pltpu.VMEM)
    outs = pl.pallas_call(
        functools.partial(kernel, n, n_dp),
        out_shape=(
            pltpu.VMEM(q_student.shape, jnp.bfloat16),
            pltpu.VMEM(q_student.shape, jnp.bfloat16),
            jax.ShapeDtypeStruct((1, 1), jnp.float32),
        ),
        in_specs=[any_spec] * 4,
        out_specs=(vmem_spec, vmem_spec, pl.BlockSpec(memory_space=pltpu.SMEM)),
        scratch_shapes=[
            pltpu.VMEM((2, rows, FEAT), jnp.bfloat16),
            pltpu.VMEM((2, GROUPS, n, 2, 8, WIDTH), jnp.bfloat16),
            pltpu.VMEM((8, HD), jnp.float32),
            pltpu.VMEM((n * n_dp, 1, HD), jnp.float32),
            dma((2,)),
            dma((2, GROUPS, 2)),
            dma((GROUPS, 2)),
            dma((GROUPS, 2)),
            dma((GROUPS, line)),
            dma((GROUPS, line)),
            dma((GROUPS, line)),
            dma((GROUPS, line)),
            dma((GROUPS, 2, line)),
            dma((GROUPS, 2, line)),
            pltpu.SemaphoreType.REGULAR,
            dma((n * n_dp,)),
            dma((n * n_dp,)),
        ],
        compiler_params=pltpu.CompilerParams(
            collective_id=0, has_side_effects=True, vmem_limit_bytes=60 * 1024 * 1024
        ),
    )(q_student, kv_student, q_target, kv_target)
    return outs[0], outs[1], outs[2].reshape(())


def solution(mesh):
    n, n_dp = mesh.shape["seq"], mesh.shape["dp"]
    spec = P("dp", "seq", None)
    return jax.shard_map(
        functools.partial(body, n, n_dp),
        mesh=mesh,
        in_specs=(spec,) * 4,
        out_specs=(spec, spec, P()),
        check_vma=False,
    )
```

time: 48.3 us -> 36.1 us (0.75)
  Pallas kernels: 43.6 us -> 31.3 us
    pallas_call x1, Pallas kernels: 43.6 us -> 31.3 us  [body(): pl.pallas_call(functools.partial(kernel, n, n_dp), out_shape=(pltpu.VMEM(...]
where the time goes in v3:
time: 36.1 us; the launch traced here: 35.9 us
  Pallas kernels  31.3 us (87%)
  between operations  2.33 us (6%)
  local copies, waits for them, and re-layouts  2.29 us (6%)
    pallas_call x1, Pallas kernels, body(): pl.pallas_call(functools.partial(kernel, n, n_dp), out_shape=(pltpu.VMEM(...  31.3 us
    unnamed x2, local copies, waits for them, and re-layouts  2.29 us

profile of v3, /device:TPU:0, one launch (start us, length us, event | category | flops | bytes accessed | tf_op | source)
XLA Modules:
  0.0 35.9 jit_solution(12028797584129645100)
XLA Ops:
  0.6 31.3 %shard_map.67 = (bf16[1,512,1536]{2,1,0:T(8,128)(2,1)S(1)}, bf16[1,512,1536]{2,1,0:T(8,128)(2,1)S(1)}, f32[1,1]{1,0:T(1,128)}) custom-call(bf16[1,512,1536]{2,1,0:T(8,128)(2,1)} %q_s.1, bf16[1,8,3072]{2,1,0:T(8,128)(2,1)} %kv_s.1, bf16[1,512,1536]{2,1,0:T(8,128)(2,1)} %q_t.1, bf16[1,8,3072]{2,1,0:T(8,128)(2,1)} %kv_t.1), custom_call_target="tpu_custom_call" | custom-call | tf_op jit(solution)/shard_map/pallas_call | solution.py:241
  32.0 1.1 %copy.10 = bf16[1,512,1536]{2,1,0:T(8,128)(2,1)} copy(bf16[1,512,1536]{2,1,0:T(8,128)(2,1)S(1)} %get-tuple-element.9) | data formatting | bytes 3145728
  33.1 1.1 %copy.11 = bf16[1,512,1536]{2,1,0:T(8,128)(2,1)} copy(bf16[1,512,1536]{2,1,0:T(8,128)(2,1)S(1)} %get-tuple-element.10) | data formatting | bytes 3145728
